TPU v7x, 256 devices: a whole 4x4x8 slice. The times are simulated.
256 devices in a mesh: section: 16 (over y, z_lo, core), tp: 16 (over z_hi, x).
Axes of the slice: x: 4, y: 4, z: 8 (z_hi: 4, z_lo: 2; z = z_hi * 2 + z_lo), core: 2. Of those that a mesh axis runs over, the one named last changes fastest.
Arguments:
- embedded: bfloat16 [768, 4096], P('tp'), may hold values from -20 to 20
- previous_out: bfloat16 [16, 768, 4096], P('section', 'tp'), may hold values from -20 to 20
- top_grad: bfloat16 [768, 4096], P('tp'), may hold values from -6 to 6
- grad_out: bfloat16 [16, 768, 4096], P('section', 'tp'), may hold values from -6 to 6
- saved_input: bfloat16 [16, 768, 4096], P('section', 'tp'), may hold values from -20 to 20
- saved_qkv: bfloat16 [16, 768, 3, 2048], P('section', None, None, 'tp'), may hold values from -64 to 64
- norm_gain: float32 [16, 2, 4096], P('section'), may hold values from 0.1 to 1.9
- qkv_weight: bfloat16 [16, 2, 4096, 3, 2048], P('section', None, None, None, 'tp'), may hold values from -4 to 4
- out_weight: bfloat16 [16, 2, 2048, 4096], P('section', None, 'tp'), may hold values from -0.125 to 0.125
- modality: int32 [16, 2, 768], P('section'), may hold values from 0 to 1, as said below
- documents: int32 [16, 2, 768], P('section'), may hold values from 0 to 3, never falling along the last dimension, each value on 1 to 384 neighbouring positions
Outputs:
- forward_out: bfloat16 [16, 768, 4096], P('section', 'tp')
- backward_out: bfloat16 [16, 768, 4096], P('section', 'tp')
Inputs may be any that keep to these rules, and one draw needn't show every extreme that they name: `modality`: 0 marks a text token and 1 an image token; image tokens come in runs of positions, and both modalities occur in every micro-batch. `documents`: document numbers start at 0 and never fall along the positions of a micro-batch.
All inputs are finite; a program needn't handle non-finite values.
Results may differ from a plain program's by a relative error of at most 0.014.
Values may be sent and summed in bfloat16 or wider, within the bound.
A program may use at most 128 MiB of HBM per device.

v0:
```python
import math

import jax
import jax.numpy as jnp
from jax import lax
from jax.sharding import PartitionSpec as P

HEAD_DIM = 128


EPSILON = 1e-05


def from_behind(block, axis, distance):
    devices = range(lax.axis_size(axis))
    route = [(i - distance, i) for i in devices if i - distance in devices]
    return lax.ppermute(block, axis, route)


def in_one_piece(arrays, axis, dim, along):
    ends, at = ([], 0)
    for a in arrays[:-1]:
        at += a.shape[along]
        ends.append(at)
    both = jnp.concatenate(arrays, axis=along)
    return tuple(jnp.split(lax.all_gather(both, axis, axis=dim, tiled=True), ends, axis=along))


def contract(rows, weights, side):
    return lax.dot_general(
        rows, weights, (((1,), (side,)), ((), ())), preferred_element_type=jnp.float32
    )


def selected(rows, labels, weights, side):
    first = contract(rows, weights[0], side)
    second = contract(rows, weights[1], side)
    return jnp.where(labels[:, None] == 0, first, second)


def project(rows, labels, weights, side):
    result = selected(rows, labels, weights, side)
    return result


def term_source(rows, labels, weights, side):

    def piece(first, row_count):
        return selected(rows, labels, weights, side)

    return piece


def gain_rows(gains, labels):
    return jnp.where(labels[:, None] == 0, gains[0][None, :], gains[1][None, :])


def probabilities(queries, keys, documents_row):
    length = queries.shape[0]
    scores = jnp.einsum(
        "thd,shd->hts", queries, keys, preferred_element_type=jnp.float32
    ) / math.sqrt(HEAD_DIM)
    position = jnp.arange(length, dtype=jnp.int32)
    allowed = (position[None, :] <= position[:, None]) & (
        documents_row[:, None] == documents_row[None, :]
    )
    scores = jnp.where(allowed[None, :, :], scores, -jnp.inf)
    highest = jnp.max(scores, axis=-1, keepdims=True)
    weights = jnp.exp(scores - highest)
    return weights / jnp.sum(weights, axis=-1, keepdims=True)


def forward_attention(normed_all, labels, documents_row, w_project, heads_here):
    length = normed_all.shape[0]
    projected = project(normed_all, labels, w_project, 0).astype(jnp.bfloat16)
    projected = projected.reshape(length, 3, heads_here, HEAD_DIM)
    probs = probabilities(projected[:, 0], projected[:, 1], documents_row).astype(jnp.bfloat16)
    attended = jnp.einsum(
        "hts,shd->thd", probs, projected[:, 2], preferred_element_type=jnp.float32
    )
    return attended.astype(jnp.bfloat16).reshape(length, heads_here * HEAD_DIM)


def backward_attention(upstream_all, labels, documents_row, w_output, saved, heads_here):
    length = upstream_all.shape[0]
    grad_attended = project(upstream_all, labels, w_output, 1).astype(jnp.bfloat16)
    grad_attended = grad_attended.reshape(length, heads_here, HEAD_DIM)
    stored = saved.reshape(length, 3, heads_here, HEAD_DIM)
    queries = stored[:, 0]
    keys = stored[:, 1]
    values = stored[:, 2]
    probs_back = probabilities(queries, keys, documents_row)
    rounded = probs_back.astype(jnp.bfloat16)
    grad_values = jnp.einsum(
        "hts,thd->shd", rounded, grad_attended, preferred_element_type=jnp.float32
    ).astype(jnp.bfloat16)
    grad_probs = jnp.einsum(
        "thd,shd->hts", grad_attended, values, preferred_element_type=jnp.float32
    )
    delta = jnp.sum(probs_back * grad_probs, axis=-1, keepdims=True)
    grad_scores = (probs_back * (grad_probs - delta) / math.sqrt(HEAD_DIM)).astype(jnp.bfloat16)
    grad_queries = jnp.einsum(
        "hts,shd->thd", grad_scores, keys, preferred_element_type=jnp.float32
    ).astype(jnp.bfloat16)
    grad_keys = jnp.einsum(
        "hts,thd->shd", grad_scores, queries, preferred_element_type=jnp.float32
    ).astype(jnp.bfloat16)
    return jnp.stack([grad_queries, grad_keys, grad_values], axis=1).reshape(
        length, 3 * heads_here * HEAD_DIM
    )


def body(
    embedded,
    previous_out,
    top_grad,
    grad_out,
    saved_input,
    saved_qkv,
    norm_gain,
    qkv_weight,
    out_weight,
    modality,
    documents,
):
    section = lax.axis_index("section")
    arrived = from_behind(previous_out[0], "section", 1)
    returned = from_behind(grad_out[0], "section", -1)
    inputs = jnp.where(section == 0, embedded, arrived)
    upstream = jnp.where(section == lax.axis_size("section") - 1, top_grad, returned)
    local = inputs.shape[0]
    width = inputs.shape[1]
    offset = lax.axis_index("tp") * local
    labels_fwd = modality[0, 0]
    labels_back = modality[0, 1]
    documents_fwd = documents[0, 0]
    documents_back = documents[0, 1]
    gains = norm_gain[0]
    heads_here = qkv_weight.shape[-1] // HEAD_DIM
    w_project = qkv_weight[0].reshape(2, width, 3 * heads_here * HEAD_DIM)
    w_output = out_weight[0]
    own_fwd = lax.dynamic_slice_in_dim(labels_fwd, offset, local, 0)
    own_back = lax.dynamic_slice_in_dim(labels_back, offset, local, 0)
    forward_rows = inputs.astype(jnp.float32)
    inverse = lax.rsqrt(jnp.mean(forward_rows * forward_rows, axis=-1, keepdims=True) + EPSILON)
    normed = (forward_rows * inverse * gain_rows(gains, own_fwd)).astype(jnp.bfloat16)
    normed_all, upstream_all = in_one_piece((normed, upstream), "tp", 0, 1)
    attended = forward_attention(normed_all, labels_fwd, documents_fwd, w_project, heads_here)
    grads_flat = backward_attention(
        upstream_all, labels_back, documents_back, w_output, saved_qkv[0], heads_here
    )
    forward_piece = term_source(attended, labels_fwd, w_output, 0)
    backward_piece = term_source(grads_flat, labels_back, w_project, 1)
    first = jnp.int32(0)
    summed = lax.psum_scatter(
        jnp.concatenate(
            [
                forward_piece(first, local * lax.axis_size("tp")),
                backward_piece(first, local * lax.axis_size("tp")),
            ],
            axis=1,
        ).astype(jnp.bfloat16),
        "tp",
        scatter_dimension=0,
        tiled=True,
    ).astype(jnp.float32)
    mixed = summed[:, :width]
    grad_normed = summed[:, width:]
    forward_out = (forward_rows + mixed).astype(jnp.bfloat16)
    back_rows = saved_input[0].astype(jnp.float32)
    inverse_back = lax.rsqrt(jnp.mean(back_rows * back_rows, axis=-1, keepdims=True) + EPSILON)
    scaled = grad_normed * gain_rows(gains, own_back)
    correction = jnp.mean(scaled * back_rows, axis=-1, keepdims=True)
    norm_grad = (
        inverse_back * scaled - back_rows * inverse_back * inverse_back * inverse_back * correction
    )
    backward_out = (upstream.astype(jnp.float32) + norm_grad).astype(jnp.bfloat16)
    return (forward_out[None], backward_out[None])


def solution(mesh):
    placed = (
        P("tp", None),
        P("section", "tp", None),
        P("tp", None),
        P("section", "tp", None),
        P("section", "tp", None),
        P("section", None, None, "tp"),
        P("section", None, None),
        P("section", None, None, None, "tp"),
        P("section", None, "tp", None),
        P("section", None, None),
        P("section", None, None),
    )
    return jax.shard_map(
        body,
        mesh=mesh,
        in_specs=placed,
        out_specs=(P("section", "tp", None), P("section", "tp", None)),
        check_vma=False,
    )
```

profile of v0, /device:TPU:25, one launch (start us, length us, event | category | flops | bytes accessed | tf_op | source)
XLA Modules:
  0.0 392.3 jit_solution(12893394495946632105)
XLA Ops:
  7.2 4.2 %collective-permute-start = (bf16[48,4096]{1,0:T(8,128)(2,1)}, bf16[48,4096]{1,0:T(8,128)(2,1)S(1)}, u32[]{:S(2)}, u32[]{:S(2)}) collective-permute-start(bf16[48,4096]{1,0:T(8,128)(2,1)} %bitcast.122), channel_id=1, source_target_pairs={{0,16},{16,32},{32,48},{48,64},{64,80},{80,96},{96,112},{112,128},... | collective-permute-start | bytes 1179656 | tf_op jit(solution)/shard_map/ppermute | solution.py:17
  11.5 1.9 collective-permute-start.1
  14.3 1.4 fusion.65
  15.7 1.8 collective-permute-done
  17.9 2.8 collective-permute-done.1
  22.6 4.9 %fusion.63 = (bf16[1,1,4096,3,128]{4,2,3,1,0:T(8,128)(2,1)}, bf16[1,1,4096,3,128]{4,2,3,1,0:T(8,128)(2,1)S(1)}) fusion(bf16[1,2,4096,3,128]{4,2,3,1,0:T(8,128)(2,1)} %param.18), kind=kLoop, calls=%fused_computation.89 | loop fusion | bytes 12582912 | tf_op jit(solution)/shard_map/slice | solution.py:37
  27.5 4.7 %copy.16 = bf16[1,1,4096,3,128]{2,4,3,1,0:T(8,128)(2,1)} copy(bf16[1,1,4096,3,128]{4,2,3,1,0:T(8,128)(2,1)} %get-tuple-element.10) | data formatting | bytes 6291456
  32.2 2.8 copy.15
  35.1 1.4 slice_reduce_fusion.1
  36.4 1.4 compare_reduce_fusion.1
  37.8 1.6 fusion.66
  40.4 131.5 %all-gather.2.cloned.1.call-done = bf16[768,8192]{1,0:T(8,128)(2,1)} async-done(((bf16[48,8192]{1,0:T(8,128)(2,1)}), bf16[768,8192]{1,0:T(8,128)(2,1)}) %all-gather.2.cloned.1.call-update) | async-done | bytes 12582928 | tf_op jit(solution)/shard_map/all_gather | solution.py:26
  171.9 5.0 %fusion = bf16[768,128]{1,0:T(8,128)(2,1)S(1)} fusion(bf16[768,8192]{1,0:T(8,128)(2,1)} %all-gather.2.cloned.1.call-done, bf16[1,2,128,4096]{3,2,1,0:T(8,128)(2,1)} %param.19), kind=kOutput, calls=%fused_computation.3 | convolution fusion | flops 805306368 | bytes 7536640 | tf_op jit(solution)/shard_map/dot_general | solution.py:30
  176.9 4.6 %fusion.29 = bf16[768,128]{1,0:T(8,128)(2,1)S(1)} fusion(bf16[768,128]{1,0:T(8,128)(2,1)S(1)} %fusion, bf16[768,8192]{1,0:T(8,128)(2,1)} %all-gather.2.cloned.1.call-done, bf16[1,2,128,4096]{3,2,1,0:T(8,128)(2,1)S(1)} %copy-done.4, pred[768]{0:T(1024)(128)(4,1)S(1)} %get-tuple-element.5), kind=kOutput, calls=%fused_computation.40 | convolution fusion | flops 805404672 | bytes 7734272 | tf_op jit(solution)/shard_map/dot_general | solution.py:30
  187.4 2.6 fusion.4
  190.1 2.7 fusion.16
  194.6 3.7 fusion.68
  198.3 3.7 select_convert_fusion
  202.1 1.8 fusion.41
  203.9 2.1 select_convert_fusion.1
  206.0 5.1 %pad_maximum_fusion = bf16[768,8192]{1,0:T(8,128)(2,1)} fusion(bf16[768,4096]{1,0:T(8,128)(2,1)S(1)} %select_convert_fusion, bf16[768,4096]{1,0:T(8,128)(2,1)S(1)} %select_convert_fusion.1), kind=kLoop, calls=%fused_computation | loop fusion | flops 25165824 | bytes 25165824 | tf_op jit(solution)/shard_map/concatenate | solution.py:156
  211.9 170.6 %reduce-scatter.2.cloned.1.call-done = bf16[48,8192]{1,0:T(8,128)(2,1)} async-done(((bf16[768,8192]{1,0:T(8,128)(2,1)}), bf16[48,8192]{1,0:T(8,128)(2,1)}) %reduce-scatter.2.cloned.1.call-update) | async-done | bytes 786448 | tf_op jit(solution)/shard_map/reduce_scatter | solution.py:155
  382.5 1.2 convert_element_type.106
  384.1 1.3 fusion.60
  (65 shorter events, 13.1 us)
Async XLA Ops:
  7.2 13.6 %copy-start.6 = (bf16[48,4096]{1,0:T(8,128)(2,1)S(1)}, bf16[48,4096]{1,0:T(8,128)(2,1)}, u32[]{:S(2)}) copy-start(bf16[48,4096]{1,0:T(8,128)(2,1)} %param.13) | copy-start | bytes 1179652
  7.2 164.7 %all-gather.2.cloned.1.call-start = ((), (), s32[]{:S(2)}) async-start(), calls=%async_computation.1 | async-start | bytes 13369344 | tf_op jit(solution)/shard_map/all_gather | solution.py:26
  7.2 10.3 %collective-permute-start = (bf16[48,4096]{1,0:T(8,128)(2,1)}, bf16[48,4096]{1,0:T(8,128)(2,1)S(1)}, u32[]{:S(2)}, u32[]{:S(2)}) collective-permute-start(bf16[48,4096]{1,0:T(8,128)(2,1)} %bitcast.122), channel_id=1, source_target_pairs={{0,16},{16,32},{32,48},{48,64},{64,80},{80,96},{96,112},{112,128},... | collective-permute-start | bytes 1179656 | tf_op jit(solution)/shard_map/ppermute | solution.py:17
  11.5 9.3 %collective-permute-start.1 = (bf16[48,4096]{1,0:T(8,128)(2,1)}, bf16[48,4096]{1,0:T(8,128)(2,1)S(1)}, u32[]{:S(2)}, u32[]{:S(2)}) collective-permute-start(bf16[48,4096]{1,0:T(8,128)(2,1)} %bitcast.123), channel_id=1, source_target_pairs={{16,0},{32,16},{48,32},{64,48},{80,64},{96,80},{112,96},{128,112},... | collective-permute-start | bytes 1179656 | tf_op jit(solution)/shard_map/ppermute | solution.py:17
  14.3 8.3 %copy-start.7 = (f32[1,1,4096]{2,1,0:T(1,128)}, f32[1,1,4096]{2,1,0:T(1,128)S(1)}, u32[]{:S(2)}) copy-start(f32[1,1,4096]{2,1,0:T(1,128)S(1)} %get-tuple-element.15) | copy-start | bytes 49156
  20.8 0.7 copy-start
  22.6 359.9 %reduce-scatter.2.cloned.1.call-start = ((), (), s32[]{:S(2)}) async-start(), calls=%async_computation.2 | async-start | bytes 13369344 | tf_op jit(solution)/shard_map/reduce_scatter | solution.py:155
  37.8 139.0 %copy-start.15 = (pred[768]{0:T(1024)(128)(4,1)}, pred[768]{0:T(1024)(128)(4,1)S(1)}, u32[]{:S(2)}) copy-start(pred[768]{0:T(1024)(128)(4,1)S(1)} %get-tuple-element.5) | copy-start | bytes 2308
  39.4 137.4 %copy-start.11 = (f32[768]{0:T(1024)}, f32[768]{0:T(1024)S(1)}, u32[]{:S(2)}) copy-start(f32[768]{0:T(1024)S(1)} %get-tuple-element.18) | copy-start | bytes 9220
  171.9 5.0 %copy-start.4 = (bf16[1,2,128,4096]{3,2,1,0:T(8,128)(2,1)S(1)}, bf16[1,2,128,4096]{3,2,1,0:T(8,128)(2,1)}, u32[]{:S(2)}) copy-start(bf16[1,2,128,4096]{3,2,1,0:T(8,128)(2,1)} %param.19) | copy-start | bytes 6291460
  176.9 4.6 %copy-start.12 = (f32[768]{0:T(1024)S(1)}, f32[768]{0:T(1024)}, u32[]{:S(2)}) copy-start(f32[768]{0:T(1024)} %copy-done.11) | copy-start | bytes 9220
  176.9 4.6 %copy-start.13 = (f32[768]{0:T(1024)S(1)}, f32[768]{0:T(1024)}, u32[]{:S(2)}) copy-start(f32[768]{0:T(1024)} %fusion.12) | copy-start | bytes 9220
  181.5 1.1 copy-start.9
  181.5 3.2 slice-start
  182.6 2.8 slice-start.1
  182.6 4.0 %slice-start.2 = ((s8[12582912]{0:T(1024)(128)(4,1)}), s8[4194304]{0:T(1024)(128)(4,1)S(1)}, s32[]{:S(2)}) async-start(s8[12582912]{0:T(1024)(128)(4,1)} %bitcast.120), calls=%async_computation.5 | async-start | bytes 8388608
  183.8 3.6 copy-start.2
  187.4 2.6 copy-start.3
  187.4 2.6 copy-start.10
  190.1 2.7 copy-start.14
  194.6 3.7 copy-start.16
  211.1 172.7 %copy-start.5 = (bf16[1,48,4096]{2,1,0:T(8,128)(2,1)S(1)}, bf16[1,48,4096]{2,1,0:T(8,128)(2,1)}, u32[]{:S(2)}) copy-start(bf16[1,48,4096]{2,1,0:T(8,128)(2,1)} %param.15) | copy-start | bytes 1179652
  211.1 172.6 %copy-start.8 = (f32[1,1,4096]{2,1,0:T(1,128)S(1)}, f32[1,1,4096]{2,1,0:T(1,128)}, u32[]{:S(2)}) copy-start(f32[1,1,4096]{2,1,0:T(1,128)} %copy-done.7) | copy-start | bytes 49156
  211.1 173.0 %copy-start.1 = (bf16[48,4096]{1,0:T(8,128)(2,1)S(1)}, bf16[48,4096]{1,0:T(8,128)(2,1)}, u32[]{:S(2)}) copy-start(bf16[48,4096]{1,0:T(8,128)(2,1)} %copy-done) | copy-start | bytes 1179652
Sparse Core Ops, SparseCore 0:
  22.7 149.1 all-gather.1
  211.2 171.2 reduce-scatter.1
where the time goes:
time: 394 us; the launch traced here: 392 us
  waiting for transfers between devices  307 us (78%)
  matrix products  31.1 us (8%)
  local copies, waits for them, and re-layouts  20 us (5%)
  between operations  14.4 us (4%)
  other arithmetic  13.8 us (4%)
  starting transfers between devices  6.24 us (2%)
    reduce_scatter x1, waiting for transfers between devices, body(): lax.psum_scatter(jnp.concatenate([forward_piece(first, local * lax.axis_s...  171 us
    all_gather x1, waiting for transfers between devices, in_one_piece(): lax.all_gather(both, axis, axis=dim, tiled=True)  131 us
    dot_general x8, matrix products, contract(): lax.dot_general(rows, weights, (((1,), (side,)), ((), ())), preferred_ele...  26.2 us
    unnamed x42, local copies, waits for them, and re-layouts  11.5 us
  transfers between devices with their start and end apart: 4, of which 4 were waited for; matrix products, arithmetic and copies ran while one was open for 5% of the time, Pallas kernels for 0%

commit v1 on v0

v1 whole, which is shorter than its diff:
```python
import functools
import math

import jax
import jax.numpy as jnp
from jax import lax
from jax.experimental import pallas as pl
from jax.experimental.pallas import tpu as pltpu
from jax.sharding import PartitionSpec as P

EPSILON = 1e-05
HEAD_DIM = 128
MESH = pl.DeviceIdType.MESH
BF = jnp.bfloat16
F32 = jnp.float32
QB = 256


def nt(x, y):
    return lax.dot_general(x, y, (((1,), (1,)), ((), ())), preferred_element_type=F32)


def tn(x, y):
    return lax.dot_general(x, y, (((0,), (0,)), ((), ())), preferred_element_type=F32)


def nn(x, y):
    return jnp.dot(x, y, preferred_element_type=F32)


class Sems:
    def __init__(self, send, recv):
        self.send, self.recv, self.count, self.open = send, recv, 0, []

    def copy(self, src, dst, peer):
        i = self.count
        self.count += 1
        c = pltpu.make_async_remote_copy(
            src_ref=src, dst_ref=dst, send_sem=self.send.at[i], recv_sem=self.recv.at[i],
            device_id=peer, device_id_type=MESH,
        )
        c.start()
        self.open.append(c)
        return i

    def landed(self, ref, i, peer):
        pltpu.make_async_remote_copy(
            src_ref=ref, dst_ref=ref, send_sem=self.send.at[i], recv_sem=self.recv.at[i],
            device_id=peer, device_id_type=MESH,
        ).wait_recv()

    def drain(self):
        for c in self.open:
            c.wait_send()


N_SEMS = 112
N_LOCAL = 16


def kernel(
    emb, prev, topg, gout, sin, sqkv, gain, wq, wo, mod, doc,
    fout, bout,
    w1, wor, inp, embv, ups, topv, sinv, qkvv, ag, proj, attg, op, oz1, oz2, fo, fa,
    u, gap, gar, gat, pb, ds, dkv, gr, g, gx1, gx2, sx, gz1, gz2, lt, dt, acc,
    ssem, rsem, lsem,
):
    s = lax.axis_index("section")
    t = lax.axis_index("tp")
    n_sec = lax.axis_size("section")
    a, b = t % 4, t // 4
    aR, aL, aO = (a + 1) % 4, (a + 3) % 4, (a + 2) % 4
    bR, bL, bO = (b + 1) % 4, (b + 3) % 4, (b + 2) % 4
    XR, XL, XO = (s, 4 * b + aR), (s, 4 * b + aL), (s, 4 * b + aO)
    ZR, ZL = (s, 4 * bR + a), (s, 4 * bL + a)
    SR, SL = ((s + 1) % n_sec, t), ((s + n_sec - 1) % n_sec, t)
    rows = inp.shape[0]
    width = inp.shape[1]
    half = width // 2
    quarter = width // 4
    length = ag.shape[0] * rows
    chunk = 4 * rows
    scale = 1.0 / math.sqrt(HEAD_DIM)

    bar = pltpu.get_barrier_semaphore()
    for peer in (SR, SL, XR, XL, XO, ZR, ZL):
        pl.semaphore_signal(bar, inc=1, device_id=peer, device_id_type=MESH)
    pl.semaphore_wait(bar, 7)

    q = Sems(ssem, rsem)
    local = []

    def fetch(src, dst):
        c = pltpu.make_async_copy(src, dst, lsem.at[len(local)])
        c.start()
        local.append(c)
        return c

    i_shift_f = q.copy(prev, inp, SR)
    i_shift_b = q.copy(gout, ups, SL)

    def regroup(m):
        mine = fetch(wo.at[m, :, pl.ds(pl.multiple_of(a * quarter, quarter), quarter)], wor.at[m, a])
        ids = []
        for peer, col in ((XR, aR), (XL, aL), (XO, aO)):
            src = wo.at[m, :, pl.ds(pl.multiple_of(col * quarter, quarter), quarter)]
            ids.append(q.copy(src, wor.at[m, a], peer))
        return mine, ids

    f_qkv = fetch(sqkv, qkvv)
    f_emb = fetch(emb, embv)
    f_top = fetch(topg, topv)
    f_sin = fetch(sin, sinv)
    wo0 = regroup(0)
    f_w1 = [
        fetch(wq.at[m, j], w1.at[:, pl.ds(m * 384 + j * 128, 128)]) for m in range(2) for j in range(3)
    ]

    for k in range(2):
        lt[k] = jnp.broadcast_to(mod[k : k + 1, :].astype(F32), (128, length)).T
        dt[k] = jnp.broadcast_to(doc[k : k + 1, :].astype(F32), (128, length)).T

    def softmax_block(qb, kb, which, i):
        n = (i + 1) * QB
        sc = nt(qb, kb) * scale
        qpos = lax.broadcasted_iota(jnp.int32, (QB, n), 0) + i * QB
        kpos = lax.broadcasted_iota(jnp.int32, (QB, n), 1)
        dq = dt[which, i * QB : (i + 1) * QB, 0:1]
        dk = doc[which : which + 1, 0:n].astype(F32)
        sc = jnp.where((kpos <= qpos) & (dq == dk), sc, -jnp.inf)
        e = jnp.exp(sc - jnp.max(sc, axis=-1, keepdims=True))
        return e / jnp.sum(e, axis=-1, keepdims=True)

    n_blocks = length // QB

    def saved_probs():
        for i in range(n_blocks):
            pb[i * QB : (i + 1) * QB, 0 : (i + 1) * QB] = softmax_block(
                qkvv[0, i * QB : (i + 1) * QB, :], qkvv[1, 0 : (i + 1) * QB, :], 1, i
            )

    f_qkv.wait()
    f_emb.wait()
    f_top.wait()

    q.landed(inp, i_shift_f, SL)

    def norm_rows(r, _):
        r0 = pl.multiple_of(r * 16, 16)
        x = jnp.where(s == 0, embv[pl.ds(r0, 16), :], inp[pl.ds(r0, 16), :])
        inp[pl.ds(r0, 16), :] = x
        x = x.astype(F32)
        inv = lax.rsqrt(jnp.mean(x * x, axis=-1, keepdims=True) + EPSILON)
        lab = lt[0, pl.ds(pl.multiple_of(t * rows + r0, 16), 16), 0:1]
        gn = jnp.where(lab == 0.0, gain[0:1, :], gain[1:2, :])
        ag[t, pl.ds(r0, 16), :] = (x * inv * gn).astype(BF)
        return 0

    lax.fori_loop(0, rows // 16, norm_rows, 0)
    i_nz = q.copy(ag.at[t], ag.at[t], ZR), q.copy(ag.at[t], ag.at[t], ZL)

    q.landed(ups, i_shift_b, SR)

    def up_rows(r, _):
        r0 = pl.multiple_of(r * 16, 16)
        x = jnp.where(s == n_sec - 1, topv[pl.ds(r0, 16), :], ups[pl.ds(r0, 16), :])
        ups[pl.ds(r0, 16), :] = x
        return 0

    lax.fori_loop(0, rows // 16, up_rows, 0)
    mine_rows = pl.ds(pl.multiple_of(a * rows, rows), rows)
    i_up = []
    for peer, col in ((XR, aR), (XL, aL), (XO, aO)):
        src = ups.at[:, pl.ds(pl.multiple_of(col * quarter, quarter), quarter)]
        i_up.append(q.copy(src, u.at[b, mine_rows, :], peer))
    u[b, mine_rows, :] = ups[:, pl.ds(pl.multiple_of(a * quarter, quarter), quarter)]
    wo1 = regroup(1)
    i_nx = {}

    def spread_x(key, slot):
        i_nx[key] = q.copy(ag.at[slot], ag.at[slot], XR), q.copy(ag.at[slot], ag.at[slot], XL)

    spread_x("B", t)
    saved_probs()

    for (i, peer, src_a) in zip(i_up, (XL, XR, XO), (aL, aR, aO)):
        q.landed(u.at[b, pl.ds(pl.multiple_of(src_a * rows, rows), rows), :], i, peer)
    i_uz = q.copy(u.at[b], u.at[b], ZR), q.copy(u.at[b], u.at[b], ZL)

    h0, h1 = pl.ds(0, half), pl.ds(half, half)
    slotL, slotR, slotO = 4 * bL + a, 4 * bR + a, 4 * bO + a
    q.landed(ag.at[slotL], i_nz[0], ZL)
    i_nzf0 = q.copy(ag.at[slotL, :, h0], ag.at[slotL, :, h0], ZR)
    spread_x("L", slotL)
    q.landed(ag.at[slotR], i_nz[1], ZR)
    i_nzf1 = q.copy(ag.at[slotR, :, h1], ag.at[slotR, :, h1], ZL)
    spread_x("R", slotR)

    i_nxf = {}

    def forward_x(key, bb):
        sl, sr = 4 * bb + aL, 4 * bb + aR
        q.landed(ag.at[sl], i_nx[key][0], XL)
        i0 = q.copy(ag.at[sl, :, h0], ag.at[sl, :, h0], XR)
        q.landed(ag.at[sr], i_nx[key][1], XR)
        i1 = q.copy(ag.at[sr, :, h1], ag.at[sr, :, h1], XL)
        i_nxf[key] = i0, i1

    def complete_x(key, bb):
        so = 4 * bb + aO
        q.landed(ag.at[so, :, h0], i_nxf[key][0], XL)
        q.landed(ag.at[so, :, h1], i_nxf[key][1], XR)

    KT = 512

    def project(bb):
        acc[...] = jnp.zeros_like(acc)

        def step(k, _):
            k0 = pl.ds(pl.multiple_of(k * KT, KT), KT)
            x = ag[pl.ds(4 * bb, 4), :, k0].reshape(chunk, KT)
            acc[...] += nn(x, w1[k0, :])
            return 0

        lax.fori_loop(0, width // KT, step, 0)
        r = pl.ds(pl.multiple_of(bb * chunk, chunk), chunk)
        lab = lt[0, r, 0:1]
        proj[r, :] = jnp.where(lab == 0.0, acc[:, 0:384], acc[:, 384:768]).astype(BF)

    forward_x("B", b)

    qh0, qh1 = pl.ds(0, quarter // 2), pl.ds(quarter // 2, quarter // 2)
    q.landed(u.at[bL], i_uz[0], ZL)
    i_uzf0 = q.copy(u.at[bL, :, qh0], u.at[bL, :, qh0], ZR)
    q.landed(u.at[bR], i_uz[1], ZR)
    i_uzf1 = q.copy(u.at[bR, :, qh1], u.at[bR, :, qh1], ZL)

    for c in f_w1:
        c.wait()
    complete_x("B", b)
    project(b)

    for mine, ids in (wo0, wo1):
        mine.wait()
    for m, (mine, ids) in enumerate((wo0, wo1)):
        for i, peer, src_a in zip(ids, (XL, XR, XO), (aL, aR, aO)):
            q.landed(wor.at[m, src_a], i, peer)

    def grad_att(bb):
        r = pl.ds(pl.multiple_of(bb * chunk, chunk), chunk)
        lab = lt[1, r, 0:1]
        x = u[bb]
        for hp in range(2):
            y0 = nt(x, wor[0, 2 * hp : 2 * hp + 2].reshape(256, quarter))
            y1 = nt(x, wor[1, 2 * hp : 2 * hp + 2].reshape(256, quarter))
            y = jnp.where(lab == 0.0, y0, y1).astype(BF)
            gap[2 * hp, r, :] = y[:, 0:128]
            gap[2 * hp + 1, r, :] = y[:, 128:256]

    grad_att(b)
    grad_att(bL)
    grad_att(bR)

    q.landed(ag.at[slotO, :, h0], i_nzf0, ZL)
    q.landed(ag.at[slotO, :, h1], i_nzf1, ZR)
    forward_x("L", bL)
    spread_x("O", slotO)

    q.landed(u.at[bO, :, qh0], i_uzf0, ZL)
    q.landed(u.at[bO, :, qh1], i_uzf1, ZR)
    grad_att(bO)
    i_ga = [q.copy(gap.at[k], gar.at[a], peer) for peer, k in ((XR, aR), (XL, aL), (XO, aO))]
    forward_x("R", bR)
    complete_x("L", bL)
    project(bL)

    for i, peer, src_a in zip(i_ga, (XL, XR, XO), (aL, aR, aO)):
        q.landed(gar.at[src_a], i, peer)

    def sum_ga(r, _):
        rr = pl.ds(pl.multiple_of(r * 64, 64), 64)
        total = gap[a, rr, :].astype(F32) + gar[aL, rr, :].astype(F32)
        total += gar[aR, rr, :].astype(F32) + gar[aO, rr, :].astype(F32)
        gat[rr, :] = total.astype(BF)
        return 0

    lax.fori_loop(0, length // 64, sum_ga, 0)

    for i in range(n_blocks):
        r = slice(i * QB, (i + 1) * QB)
        n = (i + 1) * QB
        p = pb[r, 0:n]
        gp = nt(gat[r, :], qkvv[2, 0:n, :])
        delta = jnp.sum(p * gp, axis=-1, keepdims=True)
        d = (p * (gp - delta) * scale).astype(BF)
        ds[r, 0:n] = d
        dq = nn(d, qkvv[1, 0:n, :]).astype(BF)
        lab = lt[1, r, 0:1]
        zero = jnp.zeros_like(dq)
        gr[r, 0:128] = jnp.where(lab == 0.0, dq, zero)
        gr[r, 384:512] = jnp.where(lab == 0.0, zero, dq)
    for j in range(n_blocks):
        cols = slice(j * QB, (j + 1) * QB)
        dk = jnp.zeros((QB, HEAD_DIM), F32)
        dv = jnp.zeros((QB, HEAD_DIM), F32)
        for i in range(j, n_blocks):
            r = slice(i * QB, (i + 1) * QB)
            dk += tn(ds[r, cols], qkvv[0, r, :])
            dv += tn(pb[r, cols].astype(BF), gat[r, :])
        lab = lt[1, cols, 0:1]
        zero = jnp.zeros((QB, HEAD_DIM), BF)
        gr[cols, 128:256] = jnp.where(lab == 0.0, dk.astype(BF), zero)
        gr[cols, 512:640] = jnp.where(lab == 0.0, zero, dk.astype(BF))
        gr[cols, 256:384] = jnp.where(lab == 0.0, dv.astype(BF), zero)
        gr[cols, 640:768] = jnp.where(lab == 0.0, zero, dv.astype(BF))

    def grad_in(bb):
        r = pl.ds(pl.multiple_of(bb * chunk, chunk), chunk)

        def step(k, _):
            k0 = pl.ds(pl.multiple_of(k * KT, KT), KT)
            y = nt(gr[r, :], w1[k0, :]).astype(BF)
            g[pl.ds(4 * bb, 4), :, k0] = y.reshape(4, rows, KT)
            return 0

        lax.fori_loop(0, width // KT, step, 0)

    order = [bO, bR, bL, b]
    i_gx = {}

    def gx_send(k):
        bb = order[k]
        o, l, r = 4 * bb + aO, 4 * bb + aL, 4 * bb + aR
        i_gx[k] = [
            q.copy(g.at[o, :, h0], gx1.at[k, 0], XL),
            q.copy(g.at[o, :, h1], gx1.at[k, 1], XR),
            q.copy(g.at[l, :, h1], gx2.at[k, 0, :, h1], XL),
            q.copy(g.at[r, :, h0], gx2.at[k, 1, :, h0], XR),
        ]

    def gx_pass(k):
        bb = order[k]
        l, r = 4 * bb + aL, 4 * bb + aR
        q.landed(gx1.at[k, 0], i_gx[k][0], XR)
        g[l, :, h0] = (g[l, :, h0].astype(F32) + gx1[k, 0].astype(F32)).astype(BF)
        i0 = q.copy(g.at[l, :, h0], gx2.at[k, 0, :, h0], XL)
        q.landed(gx1.at[k, 1], i_gx[k][1], XL)
        g[r, :, h1] = (g[r, :, h1].astype(F32) + gx1[k, 1].astype(F32)).astype(BF)
        i1 = q.copy(g.at[r, :, h1], gx2.at[k, 1, :, h1], XR)
        i_gx[k] += [i0, i1]

    def gx_sum(k):
        ids = i_gx[k]
        q.landed(gx2.at[k, 0, :, h1], ids[2], XR)
        q.landed(gx2.at[k, 1, :, h0], ids[3], XL)
        q.landed(gx2.at[k, 0, :, h0], ids[4], XR)
        q.landed(gx2.at[k, 1, :, h1], ids[5], XL)
        own = 4 * order[k] + a

        def step(c, _):
            c0 = pl.ds(pl.multiple_of(c * KT, KT), KT)
            total = g[own, :, c0].astype(F32) + gx2[k, 0, :, c0].astype(F32) + gx2[k, 1, :, c0].astype(F32)
            sx[k, :, c0] = total.astype(BF)
            return 0

        lax.fori_loop(0, width // KT, step, 0)

    grad_in(order[0])
    gx_send(0)

    forward_x("O", bO)
    complete_x("R", bR)
    project(bR)
    gx_pass(0)
    grad_in(order[1])
    gx_send(1)
    complete_x("O", bO)
    project(bO)

    for i in range(n_blocks):
        r = slice(i * QB, (i + 1) * QB)
        n = (i + 1) * QB
        p = softmax_block(proj[r, 0:128], proj[0:n, 128:256], 0, i).astype(BF)
        attg[a, r, :] = nn(p, proj[0:n, 256:384]).astype(BF)
    i_at = [q.copy(attg.at[a], attg.at[a], peer) for peer in (XR, XL, XO)]

    gx_pass(1)
    grad_in(order[2])
    gx_send(2)
    gx_sum(0)
    i_gz1 = [q.copy(sx.at[0, :, h0], gz1.at[0], ZL), q.copy(sx.at[0, :, h1], gz1.at[1], ZR)]

    for i, peer, src_a in zip(i_at, (XL, XR, XO), (aL, aR, aO)):
        q.landed(attg.at[src_a], i, peer)

    def out_proj(bb, k):
        r = pl.ds(pl.multiple_of(bb * chunk, chunk), chunk)
        lab = lt[0, r, 0:1]
        heads = [attg[h, r, :] for h in range(4)]
        zero = jnp.zeros((chunk, HEAD_DIM), BF)
        x = jnp.concatenate(
            [jnp.where(lab == 0.0, h, zero) for h in heads] + [jnp.where(lab == 0.0, zero, h) for h in heads], axis=1
        )
        for c in range(2):
            y = wor[:, :, :, c * 512 : (c + 1) * 512].reshape(1024, 512)
            op[k, :, c * 512 : (c + 1) * 512] = nn(x, y).astype(BF)

    out_proj(bO, 0)
    i_oz = [q.copy(op.at[0, :, qh0], oz1.at[0], ZL), q.copy(op.at[0, :, qh1], oz1.at[1], ZR)]
    out_proj(bR, 1)
    i_oz.append(q.copy(op.at[1, :, qh0], oz2.at[1, :, qh0], ZR))
    out_proj(bL, 2)
    i_oz.append(q.copy(op.at[2, :, qh1], oz2.at[0, :, qh1], ZL))
    out_proj(b, 3)

    gx_pass(2)
    grad_in(order[3])
    gx_send(3)

    gx_sum(1)
    i_gz2 = [q.copy(sx.at[1, :, h0], gz2.at[1, :, h0], ZR)]

    q.landed(oz1.at[0], i_oz[0], ZR)
    op[2, :, qh0] = (op[2, :, qh0].astype(F32) + oz1[0].astype(F32)).astype(BF)
    i_oz.append(q.copy(op.at[2, :, qh0], oz2.at[0, :, qh0], ZL))
    q.landed(oz1.at[1], i_oz[1], ZL)
    op[1, :, qh1] = (op[1, :, qh1].astype(F32) + oz1[1].astype(F32)).astype(BF)
    i_oz.append(q.copy(op.at[1, :, qh1], oz2.at[1, :, qh1], ZR))

    gx_pass(3)
    gx_sum(2)
    i_gz2.append(q.copy(sx.at[2, :, h1], gz2.at[0, :, h1], ZL))

    q.landed(gz1.at[0], i_gz1[0], ZR)
    sx[2, :, h0] = (sx[2, :, h0].astype(F32) + gz1[0].astype(F32)).astype(BF)
    i_gz2.append(q.copy(sx.at[2, :, h0], gz2.at[0, :, h0], ZL))
    q.landed(gz1.at[1], i_gz1[1], ZL)
    sx[1, :, h1] = (sx[1, :, h1].astype(F32) + gz1[1].astype(F32)).astype(BF)
    i_gz2.append(q.copy(sx.at[1, :, h1], gz2.at[1, :, h1], ZR))

    q.landed(oz2.at[1, :, qh0], i_oz[2], ZL)
    q.landed(oz2.at[0, :, qh1], i_oz[3], ZR)
    q.landed(oz2.at[0, :, qh0], i_oz[4], ZR)
    q.landed(oz2.at[1, :, qh1], i_oz[5], ZL)

    def sum_out(k, _):
        rr = pl.ds(pl.multiple_of(k * rows, rows), rows)
        total = op[3, rr, :].astype(F32) + oz2[0, rr, :].astype(F32) + oz2[1, rr, :].astype(F32)
        fo[k] = total.astype(BF)
        return 0

    lax.fori_loop(0, 4, sum_out, 0)
    i_fa = [q.copy(fo.at[k], fa.at[a], peer) for peer, k in ((XR, aR), (XL, aL), (XO, aO))]
    fa[a] = fo[a]

    f_sin.wait()
    gx_sum(3)

    for i, peer, src_a in zip(i_fa, (XL, XR, XO), (aL, aR, aO)):
        q.landed(fa.at[src_a], i, peer)
    for k in range(4):
        cols = slice(k * quarter, (k + 1) * quarter)
        fout[:, cols] = (inp[:, cols].astype(F32) + fa[k].astype(F32)).astype(BF)

    q.landed(gz2.at[1, :, h0], i_gz2[0], ZL)
    q.landed(gz2.at[0, :, h1], i_gz2[1], ZR)
    q.landed(gz2.at[0, :, h0], i_gz2[2], ZR)
    q.landed(gz2.at[1, :, h1], i_gz2[3], ZL)

    def back_rows(r, _):
        rr = pl.ds(pl.multiple_of(r * 16, 16), 16)
        total = sx[3, rr, :].astype(F32) + gz2[0, rr, :].astype(F32) + gz2[1, rr, :].astype(F32)
        lab = lt[1, pl.ds(pl.multiple_of(t * rows + r * 16, 16), 16), 0:1]
        scaled = total * jnp.where(lab == 0.0, gain[0:1, :], gain[1:2, :])
        x = sinv[rr, :].astype(F32)
        inv = lax.rsqrt(jnp.mean(x * x, axis=-1, keepdims=True) + EPSILON)
        corr = jnp.mean(scaled * x, axis=-1, keepdims=True)
        bout[rr, :] = (ups[rr, :].astype(F32) + inv * scaled - x * inv * inv * inv * corr).astype(BF)
        return 0

    lax.fori_loop(0, rows // 16, back_rows, 0)
    q.drain()


def body(
    embedded, previous_out, top_grad, grad_out, saved_input, saved_qkv, norm_gain, qkv_weight, out_weight,
    modality, documents,
):
    rows, width = embedded.shape
    length = saved_qkv.shape[1]
    blocks = length // rows
    quarter = width // 4
    wq = jnp.transpose(qkv_weight[0], (0, 2, 1, 3))
    sqkv = jnp.transpose(saved_qkv[0], (1, 0, 2))
    vm = pl.BlockSpec(memory_space=pltpu.VMEM)
    hb = pl.BlockSpec(memory_space=pl.ANY)
    v = pltpu.VMEM
    out = jax.ShapeDtypeStruct((rows, width), BF)
    chunk = 4 * rows
    fwd, bwd = pl.pallas_call(
        kernel,
        out_shape=(out, out),
        in_specs=[hb, hb, hb, hb, hb, hb, vm, hb, hb, vm, vm],
        out_specs=(vm, vm),
        scratch_shapes=[
            v((width, 768), BF),
            v((2, 4, 128, quarter), BF),
            v((rows, width), BF),
            v((rows, width), BF),
            v((rows, width), BF),
            v((rows, width), BF),
            v((rows, width), BF),
            v((3, length, HEAD_DIM), BF),
            v((blocks, rows, width), BF),
            v((length, 384), BF),
            v((4, length, HEAD_DIM), BF),
            v((4, chunk, quarter), BF),
            v((2, chunk, quarter // 2), BF),
            v((2, chunk, quarter), BF),
            v((4, rows, quarter), BF),
            v((4, rows, quarter), BF),
            v((4, chunk, quarter), BF),
            v((4, length, HEAD_DIM), BF),
            v((4, length, HEAD_DIM), BF),
            v((length, HEAD_DIM), BF),
            v((length, length), F32),
            v((length, length), BF),
            v((8, 128), F32),
            v((length, 768), BF),
            v((blocks, rows, width), BF),
            v((4, 2, rows, width // 2), BF),
            v((4, 2, rows, width), BF),
            v((4, rows, width), BF),
            v((2, rows, width // 2), BF),
            v((2, rows, width), BF),
            v((2, length, 128), F32),
            v((2, length, 128), F32),
            v((chunk, 768), F32),
            pltpu.SemaphoreType.DMA((N_SEMS,)),
            pltpu.SemaphoreType.DMA((N_SEMS,)),
            pltpu.SemaphoreType.DMA((N_LOCAL,)),
        ],
        compiler_params=pltpu.CompilerParams(
            collective_id=0, has_side_effects=True, vmem_limit_bytes=62 * 1024 * 1024
        ),
        name="relay",
    )(
        embedded, previous_out[0], top_grad, grad_out[0], saved_input[0], sqkv, norm_gain[0], wq, out_weight[0],
        modality[0], documents[0],
    )
    return fwd[None], bwd[None]


def solution(mesh):
    placed = (
        P("tp", None),
        P("section", "tp", None),
        P("tp", None),
        P("section", "tp", None),
        P("section", "tp", None),
        P("section", None, None, "tp"),
        P("section", None, None),
        P("section", None, None, None, "tp"),
        P("section", None, "tp", None),
        P("section", None, None),
        P("section", None, None),
    )
    return jax.shard_map(
        body,
        mesh=mesh,
        in_specs=placed,
        out_specs=(P("section", "tp", None), P("section", "tp", None)),
        check_vma=False,
    )
```

time: 394 us -> 194 us (0.49)
  waiting for transfers between devices: 307 us -> 0 us
  Pallas kernels: 0 us -> 186 us
  matrix products: 31.1 us -> 0 us
  local copies, waits for them, and re-layouts: 20 us -> 3.53 us
  other arithmetic: 13.8 us -> 0 us
  between operations: 14.4 us -> 0.64 us
  starting transfers between devices: 6.24 us -> 0 us
    pallas_call x0 -> x1, Pallas kernels: none -> 186 us  [body(): pl.pallas_call(kernel, out_shape=(out, out), in_specs=[hb, hb, hb, hb, hb...]
    reduce_scatter x1 -> x0, waiting for transfers between devices: 171 us -> none  [body(): lax.psum_scatter(jnp.concatenate([forward_piece(first, local * lax.axis_s...]
    all_gather x1 -> x0, waiting for transfers between devices: 131 us -> none  [in_one_piece(): lax.all_gather(both, axis, axis=dim, tiled=True)]
    dot_general x15 -> x0, matrix products: 31.1 us -> none  [the longest x8 26.2 us: contract(): lax.dot_general(rows, weights, (((1,), (side,)), ((), ())), preferred_ele...]
    slice x4 -> x0, local copies, waits for them, and re-layouts: 8.49 us -> none  [the longest x1 4.89 us: selected(): second = contract(rows, weights[1], side)]
    unnamed x42 -> x2, local copies, waits for them, and re-layouts: 11.5 us -> 3.53 us
    ppermute x2 -> x0, starting transfers between devices: 6.16 us -> none  [from_behind(): return lax.ppermute(block, axis, route)]
    concatenate x2 -> x0, other arithmetic: 6.01 us -> none  [the longest x1 5.05 us: body(): jnp.concatenate([forward_piece(first, local * lax.axis_size('tp')), backw...]
  transfers between devices with their start and end apart: 4 -> 0, of which waited for: 4 -> 0; matrix products, arithmetic and copies ran while one was open for 5% -> 0% of each run, Pallas kernels for 0% -> 0%
where the time goes in v1:
time: 194 us; the launch traced here: 190 us
  Pallas kernels  186 us (96%)
  local copies, waits for them, and re-layouts  3.53 us (2%)
    pallas_call x1, Pallas kernels, body(): pl.pallas_call(kernel, out_shape=(out, out), in_specs=[hb, hb, hb, hb, hb...  186 us

profile of v1, /device:TPU:25, one launch (start us, length us, event | category | flops | bytes accessed | tf_op | source)
XLA Modules:
  0.0 190.4 jit_solution(5663098025296734988)
XLA Ops:
  0.6 186.2 %relay.1 = (bf16[48,4096]{1,0:T(8,128)(2,1)}, bf16[48,4096]{1,0:T(8,128)(2,1)}) custom-call(bf16[48,4096]{1,0:T(8,128)(2,1)} %emb.1, bf16[48,4096]{1,0:T(8,128)(2,1)} %bitcast.18, bf16[48,4096]{1,0:T(8,128)(2,1)} %topg.1, bf16[48,4096]{1,0:T(8,128)(2,1)} %bitcast.19, bf16[48,4096]{1,0:T(8,128)(2,1)} %bitcast.20, bf16[3,768,128]{2,1,0:T(8,128)(2,1)} %bitcast.17, ...), custom_call_target="tpu_custom_call" | custom-call | tf_op jit(solution)/shard_map/relay/pallas_call | solution.py:500
  186.8 1.8 copy.15
  188.6 1.8 copy.16

commit v2 on v1

--- a/solution.py
+++ b/solution.py
@@ -13,6 +13,7 @@
 MESH = pl.DeviceIdType.MESH
 BF = jnp.bfloat16
 F32 = jnp.float32
+LATE = 8
 QB = 256
 
 
@@ -43,6 +44,21 @@
         self.open.append(c)
         return i
 
+    def copy_either(self, cond, src, other, dst, peer):
+        i = self.count
+        self.count += 1
+        yes, no = (
+            pltpu.make_async_remote_copy(
+                src_ref=x, dst_ref=dst, send_sem=self.send.at[i], recv_sem=self.recv.at[i],
+                device_id=peer, device_id_type=MESH,
+            )
+            for x in (src, other)
+        )
+        pl.when(cond)(yes.start)
+        pl.when(jnp.logical_not(cond))(no.start)
+        self.open.append(no)
+        return i
+
     def landed(self, ref, i, peer):
         pltpu.make_async_remote_copy(
             src_ref=ref, dst_ref=ref, send_sem=self.send.at[i], recv_sem=self.recv.at[i],
@@ -54,7 +70,7 @@
             c.wait_send()
 
 
-N_SEMS = 112
+N_SEMS = 144
 N_LOCAL = 16
 
 
@@ -73,7 +89,10 @@
     bR, bL, bO = (b + 1) % 4, (b + 3) % 4, (b + 2) % 4
     XR, XL, XO = (s, 4 * b + aR), (s, 4 * b + aL), (s, 4 * b + aO)
     ZR, ZL = (s, 4 * bR + a), (s, 4 * bL + a)
-    SR, SL = ((s + 1) % n_sec, t), ((s + n_sec - 1) % n_sec, t)
+    after, before = (s + 1) % n_sec, (s + n_sec - 1) % n_sec
+    SR, SL = (after, t), (before, t)
+    column = (a, aR, aL, aO)
+    SRs, SLs = [(after, 4 * b + k) for k in column], [(before, 4 * b + k) for k in column]
     rows = inp.shape[0]
     width = inp.shape[1]
     half = width // 2
@@ -83,9 +102,9 @@
     scale = 1.0 / math.sqrt(HEAD_DIM)
 
     bar = pltpu.get_barrier_semaphore()
-    for peer in (SR, SL, XR, XL, XO, ZR, ZL):
+    for peer in (*SRs, *SLs, XR, XL, XO, ZR, ZL):
         pl.semaphore_signal(bar, inc=1, device_id=peer, device_id_type=MESH)
-    pl.semaphore_wait(bar, 7)
+    pl.semaphore_wait(bar, 13)
 
     q = Sems(ssem, rsem)
     local = []
@@ -96,8 +115,12 @@
         local.append(c)
         return c
 
+    mine_rows = pl.ds(pl.multiple_of(a * rows, rows), rows)
+    i_up = []
+    for peer, k in zip(SLs, column):
+        cols = pl.ds(pl.multiple_of(k * quarter, quarter), quarter)
+        i_up.append(q.copy_either(s == 0, topg.at[:, cols], gout.at[:, cols], u.at[b, mine_rows, :], peer))
     i_shift_f = q.copy(prev, inp, SR)
-    i_shift_b = q.copy(gout, ups, SL)
 
     def regroup(m):
         mine = fetch(wo.at[m, :, pl.ds(pl.multiple_of(a * quarter, quarter), quarter)], wor.at[m, a])
@@ -112,6 +135,7 @@
     f_top = fetch(topg, topv)
     f_sin = fetch(sin, sinv)
     wo0 = regroup(0)
+    wo1 = regroup(1)
     f_w1 = [
         fetch(wq.at[m, j], w1.at[:, pl.ds(m * 384 + j * 128, 128)]) for m in range(2) for j in range(3)
     ]
@@ -157,59 +181,42 @@
         return 0
 
     lax.fori_loop(0, rows // 16, norm_rows, 0)
-    i_nz = q.copy(ag.at[t], ag.at[t], ZR), q.copy(ag.at[t], ag.at[t], ZL)
-
-    q.landed(ups, i_shift_b, SR)
-
-    def up_rows(r, _):
-        r0 = pl.multiple_of(r * 16, 16)
-        x = jnp.where(s == n_sec - 1, topv[pl.ds(r0, 16), :], ups[pl.ds(r0, 16), :])
-        ups[pl.ds(r0, 16), :] = x
-        return 0
-
-    lax.fori_loop(0, rows // 16, up_rows, 0)
-    mine_rows = pl.ds(pl.multiple_of(a * rows, rows), rows)
-    i_up = []
-    for peer, col in ((XR, aR), (XL, aL), (XO, aO)):
-        src = ups.at[:, pl.ds(pl.multiple_of(col * quarter, quarter), quarter)]
-        i_up.append(q.copy(src, u.at[b, mine_rows, :], peer))
-    u[b, mine_rows, :] = ups[:, pl.ds(pl.multiple_of(a * quarter, quarter), quarter)]
-    wo1 = regroup(1)
-    i_nx = {}
+    late = width // LATE
+    early = width - late
+    h0, h1 = pl.ds(0, half), pl.ds(half, half)
+    qh0, qh1 = pl.ds(0, quarter // 2), pl.ds(quarter // 2, quarter // 2)
+    ea = pl.ds(0, early)
+    e0, e1 = pl.ds(0, early // 2), pl.ds(early // 2, early // 2)
+    la = pl.ds(early, late)
+    l0, l1 = pl.ds(early, late // 2), pl.ds(early + late // 2, late // 2)
+    full = pl.ds(0, width)
+    parts = {"B": (full, h0, h1), "L": (ea, e0, e1), "R": (ea, e0, e1), "O": (ea, e0, e1)}
+    slotL, slotR, slotO = 4 * bL + a, 4 * bR + a, 4 * bO + a
+    quad, quadL, quadR, quadO = (pl.ds(pl.multiple_of(4 * bb, 4), 4) for bb in (b, bL, bR, bO))
+
+    def same(ref, peer):
+        return q.copy(ref, ref, peer)
+
+    i_nx, i_nxf = {}, {}
 
     def spread_x(key, slot):
-        i_nx[key] = q.copy(ag.at[slot], ag.at[slot], XR), q.copy(ag.at[slot], ag.at[slot], XL)
-
-    spread_x("B", t)
-    saved_probs()
-
-    for (i, peer, src_a) in zip(i_up, (XL, XR, XO), (aL, aR, aO)):
-        q.landed(u.at[b, pl.ds(pl.multiple_of(src_a * rows, rows), rows), :], i, peer)
-    i_uz = q.copy(u.at[b], u.at[b], ZR), q.copy(u.at[b], u.at[b], ZL)
-
-    h0, h1 = pl.ds(0, half), pl.ds(half, half)
-    slotL, slotR, slotO = 4 * bL + a, 4 * bR + a, 4 * bO + a
-    q.landed(ag.at[slotL], i_nz[0], ZL)
-    i_nzf0 = q.copy(ag.at[slotL, :, h0], ag.at[slotL, :, h0], ZR)
-    spread_x("L", slotL)
-    q.landed(ag.at[slotR], i_nz[1], ZR)
-    i_nzf1 = q.copy(ag.at[slotR, :, h1], ag.at[slotR, :, h1], ZL)
-    spread_x("R", slotR)
-
-    i_nxf = {}
+        c = parts[key][0]
+        i_nx[key] = same(ag.at[slot, :, c], XR), same(ag.at[slot, :, c], XL)
 
     def forward_x(key, bb):
         sl, sr = 4 * bb + aL, 4 * bb + aR
-        q.landed(ag.at[sl], i_nx[key][0], XL)
-        i0 = q.copy(ag.at[sl, :, h0], ag.at[sl, :, h0], XR)
-        q.landed(ag.at[sr], i_nx[key][1], XR)
-        i1 = q.copy(ag.at[sr, :, h1], ag.at[sr, :, h1], XL)
+        c, c0, c1 = parts[key]
+        q.landed(ag.at[sl, :, c], i_nx[key][0], XL)
+        i0 = same(ag.at[sl, :, c0], XR)
+        q.landed(ag.at[sr, :, c], i_nx[key][1], XR)
+        i1 = same(ag.at[sr, :, c1], XL)
         i_nxf[key] = i0, i1
 
     def complete_x(key, bb):
         so = 4 * bb + aO
-        q.landed(ag.at[so, :, h0], i_nxf[key][0], XL)
-        q.landed(ag.at[so, :, h1], i_nxf[key][1], XR)
+        c, c0, c1 = parts[key]
+        q.landed(ag.at[so, :, c0], i_nxf[key][0], XL)
+        q.landed(ag.at[so, :, c1], i_nxf[key][1], XR)
 
     KT = 512
 
@@ -227,18 +234,21 @@
         lab = lt[0, r, 0:1]
         proj[r, :] = jnp.where(lab == 0.0, acc[:, 0:384], acc[:, 384:768]).astype(BF)
 
+    i_nz = same(ag.at[t, :, ea], ZR), same(ag.at[t, :, ea], ZL)
+    spread_x("B", t)
+    saved_probs()
+
+    q.landed(ag.at[slotL, :, ea], i_nz[0], ZL)
+    i_nzf0 = same(ag.at[slotL, :, e0], ZR)
+    spread_x("L", slotL)
+    q.landed(ag.at[slotR, :, ea], i_nz[1], ZR)
+    i_nzf1 = same(ag.at[slotR, :, e1], ZL)
+    spread_x("R", slotR)
+
+    for i, peer, src_a in zip(i_up, SRs, column):
+        q.landed(u.at[b, pl.ds(pl.multiple_of(src_a * rows, rows), rows), :], i, peer)
+    i_uz = same(u.at[b], ZR), same(u.at[b], ZL)
     forward_x("B", b)
-
-    qh0, qh1 = pl.ds(0, quarter // 2), pl.ds(quarter // 2, quarter // 2)
-    q.landed(u.at[bL], i_uz[0], ZL)
-    i_uzf0 = q.copy(u.at[bL, :, qh0], u.at[bL, :, qh0], ZR)
-    q.landed(u.at[bR], i_uz[1], ZR)
-    i_uzf1 = q.copy(u.at[bR, :, qh1], u.at[bR, :, qh1], ZL)
-
-    for c in f_w1:
-        c.wait()
-    complete_x("B", b)
-    project(b)
 
     for mine, ids in (wo0, wo1):
         mine.wait()
@@ -258,21 +268,48 @@
             gap[2 * hp + 1, r, :] = y[:, 128:256]
 
     grad_att(b)
+    q.landed(ag.at[slotO, :, e0], i_nzf0, ZL)
+    q.landed(ag.at[slotO, :, e1], i_nzf1, ZR)
+    spread_x("O", slotO)
+    forward_x("L", bL)
+    forward_x("R", bR)
+    q.landed(u.at[bL], i_uz[0], ZL)
+    i_uzf0 = same(u.at[bL, :, qh0], ZR)
+    q.landed(u.at[bR], i_uz[1], ZR)
+    i_uzf1 = same(u.at[bR, :, qh1], ZL)
+    complete_x("B", b)
+    i_tz = same(ag.at[quad, :, la], ZR), same(ag.at[quad, :, la], ZL)
     grad_att(bL)
     grad_att(bR)
-
-    q.landed(ag.at[slotO, :, h0], i_nzf0, ZL)
-    q.landed(ag.at[slotO, :, h1], i_nzf1, ZR)
-    forward_x("L", bL)
-    spread_x("O", slotO)
-
+    for c in f_w1:
+        c.wait()
+    project(b)
+    forward_x("O", bO)
     q.landed(u.at[bO, :, qh0], i_uzf0, ZL)
     q.landed(u.at[bO, :, qh1], i_uzf1, ZR)
     grad_att(bO)
     i_ga = [q.copy(gap.at[k], gar.at[a], peer) for peer, k in ((XR, aR), (XL, aL), (XO, aO))]
-    forward_x("R", bR)
+    q.landed(ag.at[quadL, :, la], i_tz[0], ZL)
+    i_tzf0 = same(ag.at[quadL, :, l0], ZR)
+    q.landed(ag.at[quadR, :, la], i_tz[1], ZR)
+    i_tzf1 = same(ag.at[quadR, :, l1], ZL)
+    i_shift_b = q.copy(gout, ups, SL)
     complete_x("L", bL)
     project(bL)
+    complete_x("R", bR)
+    project(bR)
+
+    complete_x("O", bO)
+    q.landed(ag.at[quadO, :, l0], i_tzf0, ZL)
+    q.landed(ag.at[quadO, :, l1], i_tzf1, ZR)
+    project(bO)
+
+    for i in range(n_blocks):
+        r = slice(i * QB, (i + 1) * QB)
+        n = (i + 1) * QB
+        p = softmax_block(proj[r, 0:128], proj[0:n, 128:256], 0, i).astype(BF)
+        attg[a, r, :] = nn(p, proj[0:n, 256:384]).astype(BF)
+    i_at = [q.copy(attg.at[a], attg.at[a], peer) for peer in (XR, XL, XO)]
 
     for i, peer, src_a in zip(i_ga, (XL, XR, XO), (aL, aR, aO)):
         q.landed(gar.at[src_a], i, peer)
@@ -314,84 +351,79 @@
         gr[cols, 256:384] = jnp.where(lab == 0.0, dv.astype(BF), zero)
         gr[cols, 640:768] = jnp.where(lab == 0.0, zero, dv.astype(BF))
 
-    def grad_in(bb):
+    def grad_in(bb, c0, w):
         r = pl.ds(pl.multiple_of(bb * chunk, chunk), chunk)
 
         def step(k, _):
-            k0 = pl.ds(pl.multiple_of(k * KT, KT), KT)
+            k0 = pl.ds(pl.multiple_of(c0 + k * KT, KT), KT)
             y = nt(gr[r, :], w1[k0, :]).astype(BF)
             g[pl.ds(4 * bb, 4), :, k0] = y.reshape(4, rows, KT)
             return 0
 
-        lax.fori_loop(0, width // KT, step, 0)
-
-    order = [bO, bR, bL, b]
+        lax.fori_loop(0, w // KT, step, 0)
+
+    units = [
+        [(bO, 0, 0, half)],
+        [(bO, 0, half, half)],
+        [(bR, 1, 0, half)],
+        [(bL, 2, half, half)],
+        [(bR, 1, half, half)],
+        [(bL, 2, 0, half)],
+        [(b, 3, 0, half)],
+        [(b, 3, half, half)],
+    ]
     i_gx = {}
 
     def gx_send(k):
-        bb = order[k]
-        o, l, r = 4 * bb + aO, 4 * bb + aL, 4 * bb + aR
-        i_gx[k] = [
-            q.copy(g.at[o, :, h0], gx1.at[k, 0], XL),
-            q.copy(g.at[o, :, h1], gx1.at[k, 1], XR),
-            q.copy(g.at[l, :, h1], gx2.at[k, 0, :, h1], XL),
-            q.copy(g.at[r, :, h0], gx2.at[k, 1, :, h0], XR),
-        ]
+        for p, (bb, role, c0, w) in enumerate(units[k]):
+            grad_in(bb, c0, w)
+        for p, (bb, role, c0, w) in enumerate(units[k]):
+            lo, hi = pl.ds(c0, w // 2), pl.ds(c0 + w // 2, w // 2)
+            o, l, r = 4 * bb + aO, 4 * bb + aL, 4 * bb + aR
+            i_gx[k, p] = [
+                q.copy(g.at[o, :, lo], gx1.at[role, 0, :, pl.ds(c0 // 2, w // 2)], XL),
+                q.copy(g.at[o, :, hi], gx1.at[role, 1, :, pl.ds(c0 // 2, w // 2)], XR),
+                q.copy(g.at[l, :, hi], gx2.at[role, 0, :, hi], XL),
+                q.copy(g.at[r, :, lo], gx2.at[role, 1, :, lo], XR),
+            ]
 
     def gx_pass(k):
-        bb = order[k]
-        l, r = 4 * bb + aL, 4 * bb + aR
-        q.landed(gx1.at[k, 0], i_gx[k][0], XR)
-        g[l, :, h0] = (g[l, :, h0].astype(F32) + gx1[k, 0].astype(F32)).astype(BF)
-        i0 = q.copy(g.at[l, :, h0], gx2.at[k, 0, :, h0], XL)
-        q.landed(gx1.at[k, 1], i_gx[k][1], XL)
-        g[r, :, h1] = (g[r, :, h1].astype(F32) + gx1[k, 1].astype(F32)).astype(BF)
-        i1 = q.copy(g.at[r, :, h1], gx2.at[k, 1, :, h1], XR)
-        i_gx[k] += [i0, i1]
-
-    def gx_sum(k):
-        ids = i_gx[k]
-        q.landed(gx2.at[k, 0, :, h1], ids[2], XR)
-        q.landed(gx2.at[k, 1, :, h0], ids[3], XL)
-        q.landed(gx2.at[k, 0, :, h0], ids[4], XR)
-        q.landed(gx2.at[k, 1, :, h1], ids[5], XL)
-        own = 4 * order[k] + a
-
-        def step(c, _):
-            c0 = pl.ds(pl.multiple_of(c * KT, KT), KT)
-            total = g[own, :, c0].astype(F32) + gx2[k, 0, :, c0].astype(F32) + gx2[k, 1, :, c0].astype(F32)
-            sx[k, :, c0] = total.astype(BF)
-            return 0
-
-        lax.fori_loop(0, width // KT, step, 0)
-
-    grad_in(order[0])
+        for p, (bb, role, c0, w) in enumerate(units[k]):
+            lo, hi = pl.ds(c0, w // 2), pl.ds(c0 + w // 2, w // 2)
+            mid = pl.ds(c0 // 2, w // 2)
+            l, r = 4 * bb + aL, 4 * bb + aR
+            ids = i_gx[k, p]
+            q.landed(gx1.at[role, 0, :, mid], ids[0], XR)
+            g[l, :, lo] = (g[l, :, lo].astype(F32) + gx1[role, 0, :, mid].astype(F32)).astype(BF)
+            i0 = q.copy(g.at[l, :, lo], gx2.at[role, 0, :, lo], XL)
+            q.landed(gx1.at[role, 1, :, mid], ids[1], XL)
+            g[r, :, hi] = (g[r, :, hi].astype(F32) + gx1[role, 1, :, mid].astype(F32)).astype(BF)
+            i1 = q.copy(g.at[r, :, hi], gx2.at[role, 1, :, hi], XR)
+            ids += [i0, i1]
+
+    def gx_sum(k, more=None):
+        for p, (bb, role, c0, w) in enumerate(units[k]):
+            lo, hi = pl.ds(c0, w // 2), pl.ds(c0 + w // 2, w // 2)
+            ids = i_gx[k, p]
+            q.landed(gx2.at[role, 0, :, hi], ids[2], XR)
+            q.landed(gx2.at[role, 1, :, lo], ids[3], XL)
+            q.landed(gx2.at[role, 0, :, lo], ids[4], XR)
+            q.landed(gx2.at[role, 1, :, hi], ids[5], XL)
+            own = 4 * bb + a
+
+            def step(c, _):
+                cc = pl.ds(pl.multiple_of(c0 + c * KT, KT), KT)
+                total = g[own, :, cc].astype(F32) + gx2[role, 0, :, cc].astype(F32) + gx2[role, 1, :, cc].astype(F32)
+                if more is not None:
+                    total += gz1[more[p], :, pl.ds(pl.multiple_of(c * KT, KT), KT)].astype(F32)
+                sx[role, :, cc] = total.astype(BF)
+                return 0
+
+            lax.fori_loop(0, w // KT, step, 0)
+
     gx_send(0)
-
-    forward_x("O", bO)
-    complete_x("R", bR)
-    project(bR)
-    gx_pass(0)
-    grad_in(order[1])
     gx_send(1)
-    complete_x("O", bO)
-    project(bO)
-
-    for i in range(n_blocks):
-        r = slice(i * QB, (i + 1) * QB)
-        n = (i + 1) * QB
-        p = softmax_block(proj[r, 0:128], proj[0:n, 128:256], 0, i).astype(BF)
-        attg[a, r, :] = nn(p, proj[0:n, 256:384]).astype(BF)
-    i_at = [q.copy(attg.at[a], attg.at[a], peer) for peer in (XR, XL, XO)]
-
-    gx_pass(1)
-    grad_in(order[2])
     gx_send(2)
-    gx_sum(0)
-    i_gz1 = [q.copy(sx.at[0, :, h0], gz1.at[0], ZL), q.copy(sx.at[0, :, h1], gz1.at[1], ZR)]
-
-    for i, peer, src_a in zip(i_at, (XL, XR, XO), (aL, aR, aO)):
-        q.landed(attg.at[src_a], i, peer)
 
     def out_proj(bb, k):
         r = pl.ds(pl.multiple_of(bb * chunk, chunk), chunk)
@@ -405,38 +437,48 @@
             y = wor[:, :, :, c * 512 : (c + 1) * 512].reshape(1024, 512)
             op[k, :, c * 512 : (c + 1) * 512] = nn(x, y).astype(BF)
 
+    for i, peer, src_a in zip(i_at, (XL, XR, XO), (aL, aR, aO)):
+        q.landed(attg.at[src_a], i, peer)
     out_proj(bO, 0)
     i_oz = [q.copy(op.at[0, :, qh0], oz1.at[0], ZL), q.copy(op.at[0, :, qh1], oz1.at[1], ZR)]
     out_proj(bR, 1)
     i_oz.append(q.copy(op.at[1, :, qh0], oz2.at[1, :, qh0], ZR))
     out_proj(bL, 2)
     i_oz.append(q.copy(op.at[2, :, qh1], oz2.at[0, :, qh1], ZL))
+    gx_pass(0)
+    gx_send(3)
     out_proj(b, 3)
-
+    gx_pass(1)
+    gx_sum(0)
+    i_gz1 = [q.copy(sx.at[0, :, h0], gz1.at[0], ZL)]
+    gx_send(4)
     gx_pass(2)
-    grad_in(order[3])
-    gx_send(3)
-
     gx_sum(1)
-    i_gz2 = [q.copy(sx.at[1, :, h0], gz2.at[1, :, h0], ZR)]
-
+    i_gz1.append(q.copy(sx.at[0, :, h1], gz1.at[1], ZR))
+    gx_send(5)
     q.landed(oz1.at[0], i_oz[0], ZR)
     op[2, :, qh0] = (op[2, :, qh0].astype(F32) + oz1[0].astype(F32)).astype(BF)
     i_oz.append(q.copy(op.at[2, :, qh0], oz2.at[0, :, qh0], ZL))
     q.landed(oz1.at[1], i_oz[1], ZL)
     op[1, :, qh1] = (op[1, :, qh1].astype(F32) + oz1[1].astype(F32)).astype(BF)
     i_oz.append(q.copy(op.at[1, :, qh1], oz2.at[1, :, qh1], ZR))
-
     gx_pass(3)
     gx_sum(2)
+    i_gz2 = [q.copy(sx.at[1, :, h0], gz2.at[1, :, h0], ZR)]
+    gx_send(6)
+    gx_pass(4)
+    gx_sum(3)
     i_gz2.append(q.copy(sx.at[2, :, h1], gz2.at[0, :, h1], ZL))
-
+    gx_send(7)
+    gx_pass(5)
+    gx_pass(6)
+    q.landed(gz1.at[1], i_gz1[1], ZL)
+    gx_sum(4, (1,))
+    i_gz2.append(q.copy(sx.at[1, :, h1], gz2.at[1, :, h1], ZR))
+    gx_pass(7)
     q.landed(gz1.at[0], i_gz1[0], ZR)
-    sx[2, :, h0] = (sx[2, :, h0].astype(F32) + gz1[0].astype(F32)).astype(BF)
+    gx_sum(5, (0,))
     i_gz2.append(q.copy(sx.at[2, :, h0], gz2.at[0, :, h0], ZL))
-    q.landed(gz1.at[1], i_gz1[1], ZL)
-    sx[1, :, h1] = (sx[1, :, h1].astype(F32) + gz1[1].astype(F32)).astype(BF)
-    i_gz2.append(q.copy(sx.at[1, :, h1], gz2.at[1, :, h1], ZR))
 
     q.landed(oz2.at[1, :, qh0], i_oz[2], ZL)
     q.landed(oz2.at[0, :, qh1], i_oz[3], ZR)
@@ -454,7 +496,8 @@
     fa[a] = fo[a]
 
     f_sin.wait()
-    gx_sum(3)
+    gx_sum(6)
+    gx_sum(7)
 
     for i, peer, src_a in zip(i_fa, (XL, XR, XO), (aL, aR, aO)):
         q.landed(fa.at[src_a], i, peer)
@@ -462,10 +505,11 @@
         cols = slice(k * quarter, (k + 1) * quarter)
         fout[:, cols] = (inp[:, cols].astype(F32) + fa[k].astype(F32)).astype(BF)
 
+    q.landed(ups, i_shift_b, SR)
     q.landed(gz2.at[1, :, h0], i_gz2[0], ZL)
     q.landed(gz2.at[0, :, h1], i_gz2[1], ZR)
-    q.landed(gz2.at[0, :, h0], i_gz2[2], ZR)
-    q.landed(gz2.at[1, :, h1], i_gz2[3], ZL)
+    q.landed(gz2.at[1, :, h1], i_gz2[2], ZL)
+    q.landed(gz2.at[0, :, h0], i_gz2[3], ZR)
 
     def back_rows(r, _):
         rr = pl.ds(pl.multiple_of(r * 16, 16), 16)
@@ -475,7 +519,8 @@
         x = sinv[rr, :].astype(F32)
         inv = lax.rsqrt(jnp.mean(x * x, axis=-1, keepdims=True) + EPSILON)
         corr = jnp.mean(scaled * x, axis=-1, keepdims=True)
-        bout[rr, :] = (ups[rr, :].astype(F32) + inv * scaled - x * inv * inv * inv * corr).astype(BF)
+        up = jnp.where(s == n_sec - 1, topv[rr, :], ups[rr, :]).astype(F32)
+        bout[rr, :] = (up + inv * scaled - x * inv * inv * inv * corr).astype(BF)
         return 0
 
     lax.fori_loop(0, rows // 16, back_rows, 0)

time: 194 us -> 169 us (0.87); the launches traced: 190 us -> 168 us
  Pallas kernels: 186 us -> 164 us
    pallas_call x1, Pallas kernels: 186 us -> 164 us  [body(): pl.pallas_call(kernel, out_shape=(out, out), in_specs=[hb, hb, hb, hb, hb...]
where the time goes in v2:
time: 169 us; the launch traced here: 168 us
  Pallas kernels  164 us (97%)
  local copies, waits for them, and re-layouts  3.53 us (2%)
    pallas_call x1, Pallas kernels, body(): pl.pallas_call(kernel, out_shape=(out, out), in_specs=[hb, hb, hb, hb, hb...  164 us
    unnamed x2, local copies, waits for them, and re-layouts  3.53 us

profile of v2, /device:TPU:25, one launch (start us, length us, event | category | flops | bytes accessed | tf_op | source)
XLA Modules:
  0.0 168.4 jit_solution(4468886576938247274)
XLA Ops:
  0.6 164.2 %relay.1 = (bf16[48,4096]{1,0:T(8,128)(2,1)}, bf16[48,4096]{1,0:T(8,128)(2,1)}) custom-call(bf16[48,4096]{1,0:T(8,128)(2,1)} %emb.1, bf16[48,4096]{1,0:T(8,128)(2,1)} %bitcast.18, bf16[48,4096]{1,0:T(8,128)(2,1)} %topg.1, bf16[48,4096]{1,0:T(8,128)(2,1)} %bitcast.19, bf16[48,4096]{1,0:T(8,128)(2,1)} %bitcast.20, bf16[3,768,128]{2,1,0:T(8,128)(2,1)} %bitcast.17, ...), custom_call_target="tpu_custom_call" | custom-call | tf_op jit(solution)/shard_map/relay/pallas_call | solution.py:545
  164.9 1.8 %copy.15 = bf16[1,48,4096]{2,1,0:T(8,128)(2,1)} copy(bf16[1,48,4096]{2,1,0:T(8,128)(2,1)} %bitcast.22) | data formatting | bytes 786432
  166.6 1.8 %copy.16 = bf16[1,48,4096]{2,1,0:T(8,128)(2,1)} copy(bf16[1,48,4096]{2,1,0:T(8,128)(2,1)} %bitcast.21) | data formatting | bytes 786432

commit v3 on v2

--- a/solution.py
+++ b/solution.py
@@ -75,9 +75,9 @@
 
 
 def kernel(
-    emb, prev, topg, gout, sin, sqkv, gain, wq, wo, mod, doc,
+    emb, prev, topg, gout, sin, sqkv, gain_in, wq, wo, mod_in, doc_in,
     fout, bout,
-    w1, wor, inp, embv, ups, topv, sinv, qkvv, ag, proj, attg, op, oz1, oz2, fo, fa,
+    gain, mod, doc, w1, wor, inp, embv, ups, topv, sinv, qkvv, ag, proj, attg, op, oz1, oz2, fo, fa,
     u, gap, gar, gat, pb, ds, dkv, gr, g, gx1, gx2, sx, gz1, gz2, lt, dt, acc,
     ssem, rsem, lsem,
 ):
@@ -101,12 +101,6 @@
     chunk = 4 * rows
     scale = 1.0 / math.sqrt(HEAD_DIM)
 
-    bar = pltpu.get_barrier_semaphore()
-    for peer in (*SRs, *SLs, XR, XL, XO, ZR, ZL):
-        pl.semaphore_signal(bar, inc=1, device_id=peer, device_id_type=MESH)
-    pl.semaphore_wait(bar, 13)
-
-    q = Sems(ssem, rsem)
     local = []
 
     def fetch(src, dst):
@@ -114,6 +108,14 @@
         c.start()
         local.append(c)
         return c
+
+    f_small = [fetch(mod_in, mod), fetch(doc_in, doc), fetch(gain_in, gain)]
+    bar = pltpu.get_barrier_semaphore()
+    for peer in (*SRs, *SLs, XR, XL, XO, ZR, ZL):
+        pl.semaphore_signal(bar, inc=1, device_id=peer, device_id_type=MESH)
+    pl.semaphore_wait(bar, 13)
+
+    q = Sems(ssem, rsem)
 
     mine_rows = pl.ds(pl.multiple_of(a * rows, rows), rows)
     i_up = []
@@ -140,6 +142,8 @@
         fetch(wq.at[m, j], w1.at[:, pl.ds(m * 384 + j * 128, 128)]) for m in range(2) for j in range(3)
     ]
 
+    for c in f_small:
+        c.wait()
     for k in range(2):
         lt[k] = jnp.broadcast_to(mod[k : k + 1, :].astype(F32), (128, length)).T
         dt[k] = jnp.broadcast_to(doc[k : k + 1, :].astype(F32), (128, length)).T
@@ -476,9 +480,6 @@
     gx_sum(4, (1,))
     i_gz2.append(q.copy(sx.at[1, :, h1], gz2.at[1, :, h1], ZR))
     gx_pass(7)
-    q.landed(gz1.at[0], i_gz1[0], ZR)
-    gx_sum(5, (0,))
-    i_gz2.append(q.copy(sx.at[2, :, h0], gz2.at[0, :, h0], ZL))
 
     q.landed(oz2.at[1, :, qh0], i_oz[2], ZL)
     q.landed(oz2.at[0, :, qh1], i_oz[3], ZR)
@@ -494,6 +495,10 @@
     lax.fori_loop(0, 4, sum_out, 0)
     i_fa = [q.copy(fo.at[k], fa.at[a], peer) for peer, k in ((XR, aR), (XL, aL), (XO, aO))]
     fa[a] = fo[a]
+
+    q.landed(gz1.at[0], i_gz1[0], ZR)
+    gx_sum(5, (0,))
+    i_gz2.append(q.copy(sx.at[2, :, h0], gz2.at[0, :, h0], ZL))
 
     f_sin.wait()
     gx_sum(6)
@@ -538,16 +543,22 @@
     wq = jnp.transpose(qkv_weight[0], (0, 2, 1, 3))
     sqkv = jnp.transpose(saved_qkv[0], (1, 0, 2))
     vm = pl.BlockSpec(memory_space=pltpu.VMEM)
-    hb = pl.BlockSpec(memory_space=pl.ANY)
+    hb = pl.BlockSpec(memory_space=pltpu.HBM)
     v = pltpu.VMEM
     out = jax.ShapeDtypeStruct((rows, width), BF)
     chunk = 4 * rows
+    def far(x):
+        return pltpu.with_memory_space_constraint(x, pltpu.HBM)
+
     fwd, bwd = pl.pallas_call(
         kernel,
         out_shape=(out, out),
-        in_specs=[hb, hb, hb, hb, hb, hb, vm, hb, hb, vm, vm],
+        in_specs=[hb] * 11,
         out_specs=(vm, vm),
         scratch_shapes=[
+            v((2, width), F32),
+            v((2, length), jnp.int32),
+            v((2, length), jnp.int32),
             v((width, 768), BF),
             v((2, 4, 128, quarter), BF),
             v((rows, width), BF),
@@ -586,12 +597,12 @@
             pltpu.SemaphoreType.DMA((N_LOCAL,)),
         ],
         compiler_params=pltpu.CompilerParams(
-            collective_id=0, has_side_effects=True, vmem_limit_bytes=62 * 1024 * 1024
+            collective_id=0, has_side_effects=True, vmem_limit_bytes=50 * 1024 * 1024
         ),
         name="relay",
     )(
-        embedded, previous_out[0], top_grad, grad_out[0], saved_input[0], sqkv, norm_gain[0], wq, out_weight[0],
-        modality[0], documents[0],
+        far(embedded), far(previous_out[0]), far(top_grad), far(grad_out[0]), far(saved_input[0]), far(sqkv),
+        far(norm_gain[0]), far(wq), far(out_weight[0]), far(modality[0]), far(documents[0]),
     )
     return fwd[None], bwd[None]
 

time: 169 us -> 165 us (0.976)
  local copies, waits for them, and re-layouts: 3.53 us -> 1.49 us
    unnamed x2, local copies, waits for them, and re-layouts: 3.53 us -> 1.49 us
where the time goes in v3:
time: 165 us
  Pallas kernels  163 us (99%)
    pallas_call x1, Pallas kernels, body(): pl.pallas_call(kernel, out_shape=(out, out), in_specs=[hb] * 11, out_spec...  163 us

profile of v3, /device:TPU:25, one launch (start us, length us, event | category | flops | bytes accessed | tf_op | source)
XLA Modules:
  0.0 164.8 jit_solution(11270078756864512727)
XLA Ops:
  0.6 162.6 %relay.1 = (bf16[48,4096]{1,0:T(8,128)(2,1)S(1)}, bf16[48,4096]{1,0:T(8,128)(2,1)S(1)}) custom-call(bf16[48,4096]{1,0:T(8,128)(2,1)} %emb.1, bf16[48,4096]{1,0:T(8,128)(2,1)} %bitcast.20, bf16[48,4096]{1,0:T(8,128)(2,1)} %topg.1, bf16[48,4096]{1,0:T(8,128)(2,1)} %bitcast.21, bf16[48,4096]{1,0:T(8,128)(2,1)} %bitcast.22, bf16[3,768,128]{2,1,0:T(8,128)(2,1)} %bitcast.19, ...), custom_call_target="tpu_custom_call" | custom-call | tf_op jit(solution)/shard_map/relay/pallas_call | solution.py:553
  163.3 0.7 copy.15
  164.0 0.7 copy.16
